TPU v7x, 32 devices: a whole 2x2x4 slice. The times are simulated.
32 devices in a mesh: tm: 2 (over x), py: 4 (over y, core), pz: 4 (over z).
Axes of the slice: x: 2, y: 2, z: 4, core: 2. Of those that a mesh axis runs over, the one named last changes fastest.
Arguments:
- start_states: float32 [2, 3, 128, 8, 16, 128], P('tm', None, None, None, ('py', 'pz')), may hold values from -6 to 6
Outputs:
- new_states: float32 [2, 3, 128, 8, 16, 128], P('tm', None, None, None, ('py', 'pz'))
All inputs are finite; a program needn't handle non-finite values.
Results may differ from a plain program's by a relative error of at most 0.0001.
Values sent between devices are 32-bit elements; how exact they have to be, the bound alone decides.
A program may use at most 128 MiB of HBM per device.

v0:
```python
from functools import partial
import math

import jax
import jax.numpy as jnp
from jax import lax
import numpy as np
from jax.experimental import pallas as pl
from jax.experimental.pallas import tpu as pltpu
from jax.sharding import PartitionSpec as P

M = 64


viscosity = 0.03
time_step = 0.004
highest = lax.Precision.HIGHEST


def shifted(block, axis, distance):
    devices = range(lax.axis_size(axis))
    route = [(i - distance, i) for i in devices if i - distance in devices]
    return lax.ppermute(block, axis, route)


def signed_wave(places, length):
    return jnp.where(places < length // 2, places, places - length)


def rotate(values):
    halfway = values.shape[-1] // 2
    return jnp.concatenate([-values[..., halfway:], values[..., :halfway]], axis=-1)


def trig_pair(outer, inner, extent, factor):
    residue = jnp.mod(outer[:, None] * inner[None, :], extent)
    radians = residue.astype(jnp.float32) * (2.0 * math.pi / extent)
    return (jnp.cos(radians) * factor, jnp.sin(radians) * factor)


def complex_apply(cosine_part, sine_part, values, contracted, direction_sign):
    kernel = jnp.stack(
        [
            jnp.stack([cosine_part, -direction_sign * sine_part]),
            jnp.stack([direction_sign * sine_part, cosine_part]),
        ]
    )
    halfway = values.shape[-1] // 2
    split = values.reshape(values.shape[:-1] + (2, halfway))
    if contracted == 1:
        pattern = "pqok,fkaqh->foaph"
    else:
        pattern = "pqok,flkqh->floph"
    result = jnp.einsum(pattern, kernel, split, precision=highest)
    return result.reshape(result.shape[:-2] + (2 * halfway,))


def inverse_z(extent, retained):
    halfway = retained // 2
    columns = jnp.arange(retained, dtype=jnp.int32)
    harmonic = columns % halfway
    weight = jnp.where(harmonic == 0, 1.0, 2.0) * retained ** (-0.5)
    residue = jnp.mod(harmonic[:, None] * jnp.arange(extent, dtype=jnp.int32)[None, :], extent)
    radians = residue.astype(jnp.float32) * (2.0 * math.pi / extent)
    return (
        jnp.where((columns < halfway)[:, None], jnp.cos(radians), -jnp.sin(radians))
        * weight[:, None]
    )


def forward_z(extent, retained):
    halfway = retained // 2
    columns = jnp.arange(retained, dtype=jnp.int32)
    harmonic = columns % halfway
    residue = jnp.mod(jnp.arange(extent, dtype=jnp.int32)[:, None] * harmonic[None, :], extent)
    radians = residue.astype(jnp.float32) * (2.0 * math.pi / extent)
    return jnp.where((columns < halfway)[None, :], jnp.cos(radians), -jnp.sin(radians)) * (
        math.sqrt(retained) / extent
    )


def inverse_tail(portion, extent, sectioned, layout):
    count_py, count_pz, groups, member = layout
    retained = portion.shape[2]
    local_rows = retained // groups
    places = jnp.arange(retained, dtype=jnp.int32)
    owners = places // local_rows
    wave_y = signed_wave(places % local_rows * groups + owners, retained)
    points = jnp.arange(extent, dtype=jnp.int32)
    cosine_part, sine_part = trig_pair(points, wave_y, extent, retained ** (-0.5))
    along_y = complex_apply(cosine_part, sine_part, portion, 2, 1.0)
    return jnp.einsum("flyr,rz->flyz", along_y, inverse_z(extent, retained), precision=highest)


def forward_tail(portion, retained, sectioned, layout):
    count_py, count_pz, groups, member = layout
    extent = portion.shape[1]
    local_rows = extent // groups
    places = jnp.arange(extent, dtype=jnp.int32)
    points = places // local_rows * local_rows + places % local_rows
    wave_x = signed_wave(jnp.arange(retained, dtype=jnp.int32), retained)
    cosine_part, sine_part = trig_pair(wave_x, points, extent, math.sqrt(retained) / extent)
    return complex_apply(cosine_part, sine_part, portion, 1, -1.0)


def to_physical(coeffs, wavegrid, extent, resolution, layout):
    wave_x, wave_y, wave_z = wavegrid
    retained = coeffs.shape[1]
    seeds = jnp.concatenate([coeffs, wave_x * coeffs[1:3]], axis=0)
    points = jnp.arange(extent, dtype=jnp.int32)
    wave_rows = signed_wave(jnp.arange(retained, dtype=jnp.int32), retained)
    cosine_part, sine_part = trig_pair(points, wave_rows, extent, retained ** (-0.5))
    moved_x = complex_apply(cosine_part, sine_part, seeds, 1, 1.0)
    curl_x = rotate(wave_y * moved_x[2] - wave_z * moved_x[1])
    curl_y = rotate(wave_z * moved_x[0] - moved_x[4])
    curl_z = rotate(moved_x[3] - wave_y * moved_x[0])
    spread = jnp.concatenate([moved_x[:3], jnp.stack([curl_x, curl_y, curl_z])], axis=0)
    if resolution == "coarse":
        finish = partial(inverse_tail, extent=extent, sectioned=False, layout=layout)
        return finish(lax.all_to_all(spread, ("py", "pz"), split_axis=1, concat_axis=2, tiled=True))
    else:
        finish = partial(inverse_tail, extent=extent, sectioned=False, layout=layout)
        return finish(lax.all_to_all(spread, ("py", "pz"), split_axis=1, concat_axis=2, tiled=True))


def to_spectral(fields, retained, resolution, layout):
    count_py, count_pz, groups, member = layout
    extent = fields.shape[-1]
    along_z = jnp.einsum("flyz,zr->flyr", fields, forward_z(extent, retained), precision=highest)
    local_rows = retained // groups
    places = jnp.arange(retained, dtype=jnp.int32)
    wave_y = signed_wave(places % local_rows * groups + places // local_rows, retained)
    cosine_part, sine_part = trig_pair(
        wave_y, jnp.arange(extent, dtype=jnp.int32), extent, math.sqrt(retained) / extent
    )
    along_y = complex_apply(cosine_part, sine_part, along_z, 2, -1.0)
    if resolution == "coarse":
        finish = partial(forward_tail, retained=retained, sectioned=False, layout=layout)
        return finish(
            lax.all_to_all(along_y, ("py", "pz"), split_axis=2, concat_axis=1, tiled=True)
        )
    else:
        finish = partial(forward_tail, retained=retained, sectioned=False, layout=layout)
        return finish(
            lax.all_to_all(along_y, ("py", "pz"), split_axis=2, concat_axis=1, tiled=True)
        )


def wave_grid(retained, layout):
    count_py, count_pz, groups, member = layout
    places = jnp.arange(retained, dtype=jnp.int32)
    wave_x = signed_wave(places, retained).astype(jnp.float32)[:, None, None]
    local_places = jnp.arange(retained // groups, dtype=jnp.int32)
    wave_y = signed_wave(local_places * groups + member, retained).astype(jnp.float32)[
        None, :, None
    ]
    wave_z = (places % (retained // 2)).astype(jnp.float32)[None, None, :]
    return (wave_x, wave_y, wave_z)


def project(coeffs, wavegrid):
    wave_x, wave_y, wave_z = wavegrid
    squared = wave_x * wave_x + wave_y * wave_y + wave_z * wave_z
    divergence = (wave_x * coeffs[0] + wave_y * coeffs[1] + wave_z * coeffs[2]) / jnp.maximum(
        squared, 1.0
    )
    return jnp.stack(
        [
            coeffs[0] - wave_x * divergence,
            coeffs[1] - wave_y * divergence,
            coeffs[2] - wave_z * divergence,
        ]
    )


def cross_product(first_field, second_field):
    return jnp.stack(
        [
            first_field[1] * second_field[2] - first_field[2] * second_field[1],
            first_field[2] * second_field[0] - first_field[0] * second_field[2],
            first_field[0] * second_field[1] - first_field[1] * second_field[0],
        ]
    )


def advance(coeffs, resolution, layout):
    retained = coeffs.shape[1]
    extent = 3 * retained // 2
    wavegrid = wave_grid(retained, layout)
    fields = to_physical(coeffs, wavegrid, extent, resolution, layout)
    product = cross_product(fields[:3], fields[3:])
    nonlinear = to_spectral(product, retained, resolution, layout)
    wave_x, wave_y, wave_z = wavegrid
    squared = wave_x * wave_x + wave_y * wave_y + wave_z * wave_z
    damping = jnp.exp(-viscosity * time_step * squared)
    return damping * (coeffs + time_step * project(nonlinear, wavegrid))


def restrict(coeffs, kept, groups):
    halfway = kept // 2
    retained = coeffs.shape[1]
    rows_kept = jnp.concatenate([coeffs[:, :halfway], coeffs[:, retained - halfway :]], axis=1)
    local_rows = coeffs.shape[2]
    local_kept = kept // groups // 2
    rows_kept = jnp.concatenate(
        [rows_kept[:, :, :local_kept], rows_kept[:, :, local_rows - local_kept :]], axis=2
    )
    columns_half = coeffs.shape[3] // 2
    return jnp.concatenate(
        [rows_kept[..., :halfway], rows_kept[..., columns_half : columns_half + halfway]], axis=3
    )


def prolong(coeffs, retained, groups):
    components, kept, local_kept, width = coeffs.shape
    halfway = kept // 2
    zeros_x = jnp.zeros((components, retained - kept, local_kept, width), jnp.float32)
    wider = jnp.concatenate([coeffs[:, :halfway], zeros_x, coeffs[:, halfway:]], axis=1)
    local_rows = retained // groups
    split_rows = local_kept // 2
    zeros_y = jnp.zeros((components, retained, local_rows - local_kept, width), jnp.float32)
    wider = jnp.concatenate([wider[:, :, :split_rows], zeros_y, wider[:, :, split_rows:]], axis=2)
    zeros_z = jnp.zeros((components, retained, local_rows, retained // 2 - halfway), jnp.float32)
    return jnp.concatenate([wider[..., :halfway], zeros_z, wider[..., halfway:], zeros_z], axis=3)


def wave_table(length):
    places = np.arange(length)
    return np.where(places < length // 2, places, places - length)


def trig_table(outer, inner, extent):
    radians = 2.0 * np.pi / extent * np.mod(np.outer(outer, inner), extent)
    return np.cos(radians), np.sin(radians)


def split_table(table):
    table = np.asarray(table, np.float32)
    high = table.astype(jnp.bfloat16)
    low = (table - high.astype(np.float32)).astype(jnp.bfloat16)
    return high, low


def split(values):
    high = values.astype(jnp.bfloat16)
    low = (values - high.astype(jnp.float32)).astype(jnp.bfloat16)
    return high, low


def dot3(left, right):
    def dot(a, b):
        return jnp.dot(a, b, preferred_element_type=jnp.float32)

    return dot(left[0], right[0]) + dot(left[0], right[1]) + dot(left[1], right[0])


def z_tables(extent, retained):
    halfway = retained // 2
    columns = np.arange(retained)
    harmonic = columns % halfway
    cosine, sine = trig_table(harmonic, np.arange(extent), extent)
    table = np.where((columns < halfway)[:, None], cosine, -sine)
    weight = np.where(harmonic == 0, 1.0, 2.0)[:, None] * retained ** (-0.5)
    return table * weight, table.T * (math.sqrt(retained) / extent)


def plane_tables(extent, retained, groups):
    rows = retained // groups
    places = np.arange(retained)
    wave_y = wave_table(retained)[places % rows * groups + places // rows]
    cosine, sine = trig_table(np.arange(extent), wave_y, extent)
    inverse_y = np.concatenate([cosine, sine], axis=1) * retained ** (-0.5)
    forward_y = np.concatenate([cosine.T, -sine.T], axis=1) * (math.sqrt(retained) / extent)
    inverse_last, forward_last = z_tables(extent, retained)
    halfway = retained // 2
    turn = np.where(places < halfway, -1.0, 1.0)
    wave_z = (places % halfway).astype(np.float32)
    lanes = np.zeros((8, retained), np.float32)
    lanes[0], lanes[1] = turn, wave_z
    column = np.broadcast_to(wave_y[:, None], (retained, retained)).astype(np.float32)
    tables = [lanes, column]
    for table in (inverse_y, inverse_last, forward_last, forward_y):
        tables += split_table(table)
    return [jnp.asarray(t) for t in tables]


def plane_math(fields, tables):
    lanes, wave_y, iy0, iy1, iz0, iz1, fz0, fz1, fy0, fy1 = tables
    turn, wave_z = lanes[0:1, :], lanes[1:2, :]
    retained = wave_y.shape[0]
    extent = iy0.shape[0]

    def turned(values):
        return pltpu.roll(values, retained // 2, 1) * turn

    v0, v1, v2, d1, d2 = fields
    i0 = turned(v0)
    w0 = turned(wave_y * v2 - wave_z * v1)
    w1 = wave_z * i0 - d2
    w2 = d1 - wave_y * i0
    six = (v0, v1, v2, w0, w1, w2)
    stacked = jnp.concatenate(
        [jnp.concatenate(six, axis=1), jnp.concatenate([i0] + [turned(f) for f in six[1:]], axis=1)],
        axis=0,
    )
    along_y = dot3((iy0, iy1), split(stacked))
    rows = jnp.concatenate(
        [along_y[:, f * retained : (f + 1) * retained] for f in range(6)], axis=0
    )
    physical = dot3(split(rows), (iz0, iz1))
    u0, u1, u2, w0, w1, w2 = [physical[f * extent : (f + 1) * extent] for f in range(6)]
    product = jnp.concatenate([u1 * w2 - u2 * w1, u2 * w0 - u0 * w2, u0 * w1 - u1 * w0], axis=0)
    along_z = dot3(split(product), (fz0, fz1))
    parts = [along_z[f * extent : (f + 1) * extent] for f in range(3)]
    stacked = jnp.concatenate(
        [jnp.concatenate(parts, axis=1), jnp.concatenate([turned(p) for p in parts], axis=1)],
        axis=0,
    )
    result = dot3((fy0, fy1), split(stacked))
    return [result[:, f * retained : (f + 1) * retained] for f in range(3)]


def x_tables(extent, retained, halves):
    wave_x = wave_table(retained)
    cosine, sine = trig_table(np.arange(extent), wave_x, extent)
    values = np.concatenate([cosine, sine], axis=1)
    slopes = np.concatenate([-sine * wave_x, cosine * wave_x], axis=1)
    per_half = [table.reshape(halves, extent // halves, -1) for table in (values, slopes)]
    table = np.concatenate(per_half, axis=1) * retained ** (-0.5)
    return [jnp.asarray(t) for t in split_table(table)]


def step_kernel(*refs):
    state, x0, x1 = refs[:3]
    table_refs = refs[3:13]
    out, earlier = refs[13:15]
    spread, recv, result = refs[15:18]
    state_send, state_recv, field_send, field_recv, back_send, back_recv = refs[18:]
    _, planes, groups, rows, retained = spread.shape
    count_pz = lax.axis_size("pz")
    position = lax.axis_index("tm")
    row, place = lax.axis_index("py"), lax.axis_index("pz")
    member = row * count_pz + place
    half_points = planes * groups

    def remote(source, target, send_sem, recv_sem, half, to_member):
        return pltpu.make_async_remote_copy(
            src_ref=source,
            dst_ref=target,
            send_sem=send_sem,
            recv_sem=recv_sem,
            device_id={"tm": half, "py": to_member // count_pz, "pz": lax.rem(to_member, count_pz)},
            device_id_type=pl.DeviceIdType.MESH,
        )

    def state_copy(f):
        return remote(state.at[f], earlier.at[f], state_send.at[f], state_recv.at[f], 1, member)

    @pl.when(position == 0)
    def _():
        for f in (1, 2, 0):
            state_copy(f).start()
        earlier[...] = state[...]

    turn = table_refs[0][0:1, :]
    tables_x = (x0[position], x1[position])
    for group, f in enumerate((1, 2, 0)):
        first, count = 2 * group, 2 if f else 1

        @pl.when(position == 1)
        def _():
            state_copy(f).wait_recv()

        parts = [earlier[f, a] for a in range(rows)]
        stacked = jnp.concatenate(
            [
                jnp.concatenate(parts, axis=1),
                jnp.concatenate([pltpu.roll(p, retained // 2, 1) * turn for p in parts], axis=1),
            ],
            axis=0,
        )
        moved = dot3([t[: count * half_points] for t in tables_x], split(stacked))
        for c in range(count):
            flat = spread.at[first + c].reshape(half_points * rows, retained)
            for a in range(rows):
                flat[pl.ds(a, half_points, stride=rows), :] = moved[
                    c * half_points : (c + 1) * half_points, a * retained : (a + 1) * retained
                ]
        recv[first : first + count, :, member] = spread[first : first + count, :, member]

        def push(step, carry, first=first, count=count, group=group):
            to_member = lax.rem(member + step, groups)
            remote(
                spread.at[pl.ds(first, count), :, to_member],
                recv.at[pl.ds(first, count), :, member],
                field_send,
                field_recv.at[group],
                position,
                to_member,
            ).start()
            return carry

        lax.fori_loop(1, groups, push, 0)

    for group in range(3):
        some = recv.at[pl.ds(2 * group, 2 if group < 2 else 1), :, pl.ds(0, groups - 1)]
        remote(some, some, field_send, field_recv.at[group], position, member).wait_recv()

    tables = [ref[...] for ref in table_refs]

    def plane(p, carry):
        v1, d1, v2, d2, v0 = [recv[f, p].reshape(groups * rows, retained) for f in range(5)]
        for f, values in enumerate(plane_math([v0, v1, v2, d1, d2], tables)):
            result[p, :, f] = values.reshape(groups, rows, retained)

        def push(step, carry):
            to_member = lax.rem(member + step, groups)

            @pl.when(jnp.logical_or(position == 0, step > 0))
            def _():
                remote(
                    result.at[p, to_member],
                    out.at[position, p, member],
                    back_send,
                    back_recv,
                    1,
                    to_member,
                ).start()

            return carry

        lax.fori_loop(0, groups, push, 0)

        @pl.when(position == 1)
        def _():
            pltpu.make_async_copy(result.at[p, member], out.at[1, p, member], back_recv).start()

        return carry

    lax.fori_loop(0, planes, plane, 0)

    some = spread.at[:, :, pl.ds(0, groups - 1)]
    remote(some, some, field_send, field_recv.at[0], position, member).wait_send()

    @pl.when(position == 0)
    def _():
        for f in range(3):
            state_copy(f).wait_send()
        remote(result, result, back_send, back_recv, 1, member).wait_send()

    @pl.when(position == 1)
    def _():
        some = result.at[:, pl.ds(0, groups - 1)]
        remote(some, some, back_send, back_recv, 1, member).wait_send()
        remote(out, out, back_send, back_recv, 1, member).wait_recv()


def helped_advance(state, wavegrid, groups, halves):
    wave_x, wave_y, wave_z = wavegrid
    retained = state.shape[-1]
    rows = state.shape[2]
    extent = 3 * retained // 2
    planes = extent // (groups * halves)
    tables = x_tables(extent, retained, halves) + plane_tables(extent, retained, groups)
    vmem = pl.BlockSpec(memory_space=pltpu.VMEM)
    turned_state = jnp.swapaxes(state, 1, 2)
    arrived, earlier = pl.pallas_call(
        step_kernel,
        in_specs=[vmem] * (1 + len(tables)),
        out_specs=[pl.BlockSpec(memory_space=pl.ANY), vmem],
        out_shape=[
            jax.ShapeDtypeStruct((halves, planes, groups, 3, rows, retained), jnp.float32),
            jax.ShapeDtypeStruct(turned_state.shape, jnp.float32),
        ],
        scratch_shapes=[
            pltpu.VMEM((5, planes, groups, rows, retained), jnp.float32),
            pltpu.VMEM((5, planes, groups, rows, retained), jnp.float32),
            pltpu.VMEM((planes, groups, 3, rows, retained), jnp.float32),
            pltpu.SemaphoreType.DMA((3,)),
            pltpu.SemaphoreType.DMA((3,)),
            pltpu.SemaphoreType.DMA,
            pltpu.SemaphoreType.DMA((3,)),
            pltpu.SemaphoreType.DMA,
            pltpu.SemaphoreType.DMA,
        ],
        compiler_params=pltpu.CompilerParams(
            has_side_effects=True, vmem_limit_bytes=56 * 1024 * 1024
        ),
        name="step",
    )(turned_state, *tables)
    earlier = jnp.swapaxes(earlier, 1, 2)
    arrived = arrived.reshape(extent, 3, rows, retained)
    cosine, sine = trig_table(wave_table(retained), np.arange(extent), extent)
    forward_x = np.concatenate([cosine, -sine], axis=1) * (math.sqrt(retained) / extent)
    both = jnp.concatenate([arrived, rotate(arrived)], axis=0)
    nonlinear = jnp.einsum(
        "kx,xfar->fkar", jnp.asarray(forward_x, jnp.float32), both, precision=lax.Precision.HIGH
    )
    squared = wave_x * wave_x + wave_y * wave_y + wave_z * wave_z
    damping = jnp.exp(-viscosity * time_step * squared)
    return damping * project(earlier + time_step * nonlinear, wavegrid)


def shards(start_states):
    count_py = lax.axis_size("py")
    count_pz = lax.axis_size("pz")
    groups = count_py * count_pz
    member = lax.axis_index("py") * count_pz + lax.axis_index("pz")
    layout = (count_py, count_pz, groups, member)
    position = lax.axis_index("tm")
    slices = lax.axis_size("tm")
    retained = start_states.shape[-1]
    stored = start_states.reshape(3, retained, start_states.shape[3], retained)
    spectral_state = project(stored, wave_grid(retained, layout))
    if slices == 2:
        earlier_end = helped_advance(
            spectral_state, wave_grid(retained, layout), groups, slices
        )
        result = jnp.where(position == 0, spectral_state, earlier_end)
        return result.reshape(1, result.shape[0], retained, result.shape[2], 1, retained)
    fine_end = advance(spectral_state, "fine", layout)
    coarse_start = restrict(spectral_state, M, groups)
    coarse_next = advance(coarse_start, "coarse", layout)
    fine_low = restrict(fine_end, M, groups)
    correction = fine_low - coarse_next

    def relay(chained):
        return shifted(chained, "tm", 1)

    current = jnp.where(position == 1, relay(fine_low), coarse_start)

    def sweep_turn(turn_index, current):
        candidate = advance(current, "coarse", layout) + correction
        arrived = relay(candidate)
        return jnp.where(position == turn_index + 1, arrived, current)

    current = lax.fori_loop(1, slices - 1, sweep_turn, current)
    upper_band = fine_end - prolong(fine_low, retained, groups)
    previous = shifted(upper_band, "tm", 1)
    updated = prolong(current, retained, groups) + previous
    result = jnp.where(position == 0, spectral_state, updated)
    return result.reshape(1, result.shape[0], retained, result.shape[2], 1, retained)


def solution(mesh):
    in_specs = (P("tm", None, None, None, ("py", "pz"), None),)
    out_specs = P("tm", None, None, None, ("py", "pz"), None)
    return jax.shard_map(shards, mesh=mesh, in_specs=in_specs, out_specs=out_specs, check_vma=False)
```

profile of v0, /device:TPU:11, one launch (start us, length us, event | category | flops | bytes accessed | tf_op | source)
XLA Modules:
  0.0 115.8 jit_solution(11497544438821383553)
XLA Ops:
  0.0 0.1 broadcast_add_fusion
  0.1 2.4 %fusion.18 = (f32[1,1,128,8,1,128]{5,4,3,2,1,0:T(1,128)S(1)}, f32[1,1,128,8,1,128]{5,4,3,2,1,0:T(1,128)S(1)}, f32[1,1,128,8,1,128]{5,4,3,2,1,0:T(1,128)S(1)}) fusion(f32[1,3,128,8,1,128]{5,4,3,2,1,0:T(1,128)} %param.14), kind=kLoop, calls=%fused_computation.41 | loop fusion | bytes 3145728 | tf_op jit(solution)/shard_map/slice | solution.py:169
  2.5 0.0 copy-start
  2.6 0.0 copy-start.2
  2.6 0.0 copy-start.4
  2.6 0.5 bitcast_subtract_fusion.2
  3.1 0.3 copy-done
  3.3 0.2 copy-done.2
  3.5 0.2 copy-done.4
  3.7 1.3 %maximum_bitcast_fusion.refs_0_ = f32[3,8,128,128]{3,2,1,0:T(8,128)} fusion(f32[1,128,8,128]{3,1,2,0:T(8,128)S(1)} %get-tuple-element.16, f32[1,128,8,128]{3,1,2,0:T(8,128)S(1)} %get-tuple-element.17, f32[1,128,8,128]{3,1,2,0:T(8,128)S(1)} %get-tuple-element.15), kind=kLoop, calls=%fused_computation.8 | loop fusion | flops 786432 | bytes 3145728 | tf_op jit(solution)/shard_map/transpose | solution.py:466
  5.0 96.8 %step.1 = (f32[2,6,16,3,8,128]{5,4,3,2,1,0:T(8,128)}, f32[3,8,128,128]{3,2,1,0:T(8,128)}) custom-call(f32[3,8,128,128]{3,2,1,0:T(8,128)} %maximum_bitcast_fusion.refs_0_, bf16[2,192,256]{2,1,0:T(8,128)(2,1)} %constant.76.clone.refs_1_, bf16[2,192,256]{2,1,0:T(8,128)(2,1)} %constant.77.clone.refs_2_, f32[8,128]{1,0:T(8,128)} %constant.78.clone.refs_3_, ...), custom_call_target="tpu_custom_call" | custom-call | tf_op jit(solution)/shard_map/step/pallas_call | solution.py:467
  101.9 2.4 %copy.20 = f32[192,3,8,128]{0,3,2,1:T(8,128)S(1)} copy(f32[192,3,8,128]{3,2,1,0:T(8,128)} %bitcast.54) | data formatting | bytes 4718592 | tf_op jit(solution)/shard_map/reshape | solution.py:492
  104.3 0.0 copy-start.6
  104.3 0.0 copy-start.7
  104.3 0.2 slice_negate_fusion
  104.5 1.2 %copy-done.6 = f32[3,8,128,128]{3,2,1,0:T(8,128)S(1)} copy-done((f32[3,8,128,128]{3,2,1,0:T(8,128)S(1)}, f32[3,8,128,128]{3,2,1,0:T(8,128)}, u32[]{:S(2)}) %copy-start.6) | copy-done | bytes 1572888
  105.7 0.0 copy-done.7
  105.7 2.9 %bitcast_add_fusion = f32[3,128,8,128]{3,1,2,0:T(8,128)S(1)} fusion(f32[3,8,128,128]{3,2,1,0:T(8,128)S(1)} %copy-done.6, f32[128,384,1,1]{1,0,3,2:T(8,128)S(1)} %copy-done.7, f32[192,3,8,64]{0,3,2,1:T(8,128)S(1)} %get-tuple-element.12, f32[192,3,8,64]{0,3,2,1:T(8,128)S(1)} %get-tuple-element.11, f32[192,3,8,128]{0,3,2,1:T(8,128)S(1)} %copy.20), kind=kOutput, calls=%fused_computation.10 | convolution fusion | flops 909115392 | bytes 8060928 | tf_op jit(solution)/shard_map/kx,xfar->fkar/dot_general | solution.py:496
  108.6 0.3 subtract_bitcast_fusion.2
  108.9 0.0 copy-start.1
  108.9 0.0 copy-start.3
  108.9 0.0 copy-start.5
  108.9 0.2 subtract_bitcast_fusion.1
  109.1 0.9 copy-done.1
  109.9 0.2 copy-done.3
  110.1 0.2 copy-done.5
  110.2 1.3 %multiply_subtract_fusion.2 = (f32[1,1,128,8,1,128]{5,2,3,4,1,0:T(8,128)S(1)}, f32[1,1,128,8,1,128]{5,2,3,4,1,0:T(8,128)S(1)}, f32[1,1,128,8,1,128]{5,2,3,4,1,0:T(8,128)}) fusion(f32[1,1,128,8,1,128]{5,4,3,2,1,0:T(1,128)S(1)} %copy-done.1, f32[128]{0:T(128)S(1)} %get-tuple-element.25, f32[128]{0:T(128)S(1)} %fusion.15, f32[128,8]{0,1:T(8,128)S(1)} %broadcast_add_fusion, ...), kind=kLoop, calls=%fused_computation.28 | loop fusion | flops 1835008 | bytes 3151392 | tf_op jit(solution)/shard_map/sub | solution.py:169
  111.5 0.2 multiply_exponential_fusion
  111.7 1.3 %maximum_select_fusion = f32[1,3,128,8,1,128]{5,2,3,4,1,0:T(8,128)S(1)} fusion(f32[1,1,128,8,1,128]{5,2,3,4,1,0:T(8,128)S(1)} %get-tuple-element.19, f32[1,1,128,8,1,128]{5,2,3,4,1,0:T(8,128)} %get-tuple-element.20, f32[1,1,128,8,1,128]{5,2,3,4,1,0:T(8,128)S(1)} %get-tuple-element.18, f32[1,1,128,8,1,128]{5,2,3,4,1,0:T(8,128)S(1)} %get-tuple-element.14, ...), kind=kLoop, calls=%fused_computation.7 | loop fusion | flops 2359296 | bytes 5242881 | tf_op jit(solution)/shard_map/jit(_where)/select_n | solution.py:519
  113.0 2.8 %copy.22 = f32[1,3,128,8,1,128]{5,4,3,2,1,0:T(1,128)} copy(f32[1,3,128,8,1,128]{5,2,3,4,1,0:T(8,128)S(1)} %maximum_select_fusion) | data formatting | bytes 3145728 | tf_op jit(solution)/shard_map/jit(_where)/select_n | solution.py:519
  (5 shorter events, 0.0 us)
Async XLA Ops:
  2.5 0.8 copy-start
  2.6 1.0 copy-start.2
  2.6 1.2 %copy-start.4 = (f32[1,1,128,8,1,128]{5,4,3,2,1,0:T(1,128)}, f32[1,1,128,8,1,128]{5,4,3,2,1,0:T(1,128)S(1)}, u32[]{:S(2)}) copy-start(f32[1,1,128,8,1,128]{5,4,3,2,1,0:T(1,128)S(1)} %get-tuple-element.23) | copy-start | bytes 1572868
  104.3 1.4 %copy-start.6 = (f32[3,8,128,128]{3,2,1,0:T(8,128)S(1)}, f32[3,8,128,128]{3,2,1,0:T(8,128)}, u32[]{:S(2)}) copy-start(f32[3,8,128,128]{3,2,1,0:T(8,128)} %get-tuple-element.7) | copy-start | bytes 4718596
  104.3 1.4 %copy-start.7 = (f32[128,384,1,1]{1,0,3,2:T(8,128)S(1)}, f32[128,384,1,1]{1,0,3,2:T(8,128)}, u32[]{:S(2)}) copy-start(f32[128,384,1,1]{1,0,3,2:T(8,128)} %constant.90) | copy-start | bytes 589828
  108.9 1.0 copy-start.1
  108.9 1.2 %copy-start.3 = (f32[1,1,128,8,1,128]{5,4,3,2,1,0:T(1,128)S(1)}, f32[1,1,128,8,1,128]{5,4,3,2,1,0:T(1,128)}, u32[]{:S(2)}) copy-start(f32[1,1,128,8,1,128]{5,4,3,2,1,0:T(1,128)} %copy-done.2) | copy-start | bytes 1572868
  108.9 1.3 %copy-start.5 = (f32[1,1,128,8,1,128]{5,4,3,2,1,0:T(1,128)S(1)}, f32[1,1,128,8,1,128]{5,4,3,2,1,0:T(1,128)}, u32[]{:S(2)}) copy-start(f32[1,1,128,8,1,128]{5,4,3,2,1,0:T(1,128)} %copy-done.4) | copy-start | bytes 1572868
where the time goes:
time: 117 us; the launch traced here: 116 us
  Pallas kernels  96.8 us (83%)
  local copies, waits for them, and re-layouts  10.6 us (9%)
  other arithmetic  5.29 us (5%)
  matrix products  2.9 us (2%)
    pallas_call x1, Pallas kernels, helped_advance(): pl.pallas_call(step_kernel, in_specs=[vmem] * (1 + len(tables)), out_spec...  96.8 us
    unnamed x16, local copies, waits for them, and re-layouts  3.03 us
    dot_general x1, matrix products, helped_advance(): jnp.einsum('kx,xfar->fkar', jnp.asarray(forward_x, jnp.float32), both, pr...  2.9 us
    select_n x1, local copies, waits for them, and re-layouts, shards(): result = jnp.where(position == 0, spectral_state, earlier_end)  2.76 us
    slice x1, local copies, waits for them, and re-layouts, project(): coeffs[0] - wave_x * divergence  2.44 us
    reshape x1, local copies, waits for them, and re-layouts, helped_advance(): arrived = arrived.reshape(extent, 3, rows, retained)  2.39 us

commit v1 on v0

--- a/solution.py
+++ b/solution.py
@@ -353,6 +353,13 @@
             device_id_type=pl.DeviceIdType.MESH,
         )
 
+    count_py = lax.axis_size("py")
+    early = planes // 2
+
+    def far_first(step):
+        to_place = lax.rem(place + count_pz // 2 + step // count_py, count_pz)
+        return lax.rem(row + lax.rem(step, count_py), count_py) * count_pz + to_place
+
     def state_copy(f):
         return remote(state.at[f], earlier.at[f], state_send.at[f], state_recv.at[f], 1, member)
 
@@ -388,35 +395,51 @@
                 ]
         recv[first : first + count, :, member] = spread[first : first + count, :, member]
 
-        def push(step, carry, first=first, count=count, group=group):
-            to_member = lax.rem(member + step, groups)
-            remote(
-                spread.at[pl.ds(first, count), :, to_member],
-                recv.at[pl.ds(first, count), :, member],
-                field_send,
-                field_recv.at[group],
-                position,
-                to_member,
-            ).start()
-            return carry
-
-        lax.fori_loop(1, groups, push, 0)
-
-    for group in range(3):
-        some = recv.at[pl.ds(2 * group, 2 if group < 2 else 1), :, pl.ds(0, groups - 1)]
-        remote(some, some, field_send, field_recv.at[group], position, member).wait_recv()
+        batches = [(group, 0, planes)] if f else [(group, 0, early), (group + 1, early, planes)]
+        for batch, start, stop in batches:
+
+            def push(step, carry, first=first, count=count, batch=batch, start=start, stop=stop):
+                to_member = far_first(step)
+                fields, span = pl.ds(first, count), pl.ds(start, stop - start)
+
+                @pl.when(to_member != member)
+                def _():
+                    remote(
+                        spread.at[fields, span, to_member],
+                        recv.at[fields, span, member],
+                        field_send,
+                        field_recv.at[batch],
+                        position,
+                        to_member,
+                    ).start()
+
+                return carry
+
+            lax.fori_loop(0, groups, push, 0)
+
+    def await_fields(batch, first, count, start, stop):
+        some = recv.at[pl.ds(first, count), pl.ds(start, stop - start), pl.ds(0, groups - 1)]
+        remote(some, some, field_send, field_recv.at[batch], position, member).wait_recv()
+
+    await_fields(0, 0, 2, 0, planes)
+    await_fields(1, 2, 2, 0, planes)
+    await_fields(2, 4, 1, 0, early)
 
     tables = [ref[...] for ref in table_refs]
 
     def plane(p, carry):
+        @pl.when(p == early)
+        def _():
+            await_fields(3, 4, 1, early, planes)
+
         v1, d1, v2, d2, v0 = [recv[f, p].reshape(groups * rows, retained) for f in range(5)]
         for f, values in enumerate(plane_math([v0, v1, v2, d1, d2], tables)):
             result[p, :, f] = values.reshape(groups, rows, retained)
 
         def push(step, carry):
-            to_member = lax.rem(member + step, groups)
-
-            @pl.when(jnp.logical_or(position == 0, step > 0))
+            to_member = far_first(step)
+
+            @pl.when(jnp.logical_or(position == 0, to_member != member))
             def _():
                 remote(
                     result.at[p, to_member],
@@ -479,7 +502,7 @@
             pltpu.SemaphoreType.DMA((3,)),
             pltpu.SemaphoreType.DMA((3,)),
             pltpu.SemaphoreType.DMA,
-            pltpu.SemaphoreType.DMA((3,)),
+            pltpu.SemaphoreType.DMA((4,)),
             pltpu.SemaphoreType.DMA,
             pltpu.SemaphoreType.DMA,
         ],

time: 117 us -> 115 us (0.983)
  Pallas kernels: 96.8 us -> 94.9 us
    pallas_call x1, Pallas kernels: 96.8 us -> 94.9 us  [helped_advance(): pl.pallas_call(step_kernel, in_specs=[vmem] * (1 + len(tables)), out_spec...]
where the time goes in v1:
time: 115 us; the launch traced here: 114 us
  Pallas kernels  94.9 us (83%)
  local copies, waits for them, and re-layouts  10.6 us (9%)
  other arithmetic  5.29 us (5%)
  matrix products  2.89 us (3%)
    pallas_call x1, Pallas kernels, helped_advance(): pl.pallas_call(step_kernel, in_specs=[vmem] * (1 + len(tables)), out_spec...  94.9 us
    unnamed x16, local copies, waits for them, and re-layouts  3.03 us
    dot_general x1, matrix products, helped_advance(): jnp.einsum('kx,xfar->fkar', jnp.asarray(forward_x, jnp.float32), both, pr...  2.89 us
    select_n x1, local copies, waits for them, and re-layouts, shards(): result = jnp.where(position == 0, spectral_state, earlier_end)  2.76 us
    slice x1, local copies, waits for them, and re-layouts, project(): coeffs[0] - wave_x * divergence  2.44 us
    reshape x1, local copies, waits for them, and re-layouts, helped_advance(): arrived = arrived.reshape(extent, 3, rows, retained)  2.39 us

profile of v1, /device:TPU:11, one launch (start us, length us, event | category | flops | bytes accessed | tf_op | source)
XLA Modules:
  0.0 113.9 jit_solution(6751539808886253336)
XLA Ops:
  0.0 0.1 broadcast_add_fusion
  0.1 2.4 %fusion.18 = (f32[1,1,128,8,1,128]{5,4,3,2,1,0:T(1,128)S(1)}, f32[1,1,128,8,1,128]{5,4,3,2,1,0:T(1,128)S(1)}, f32[1,1,128,8,1,128]{5,4,3,2,1,0:T(1,128)S(1)}) fusion(f32[1,3,128,8,1,128]{5,4,3,2,1,0:T(1,128)} %param.14), kind=kLoop, calls=%fused_computation.41 | loop fusion | bytes 3145728 | tf_op jit(solution)/shard_map/slice | solution.py:169
  2.5 0.0 copy-start
  2.6 0.0 copy-start.2
  2.6 0.0 copy-start.4
  2.6 0.5 bitcast_subtract_fusion.2
  3.1 0.3 copy-done
  3.3 0.2 copy-done.2
  3.5 0.2 copy-done.4
  3.7 1.3 %maximum_bitcast_fusion.refs_0_ = f32[3,8,128,128]{3,2,1,0:T(8,128)} fusion(f32[1,128,8,128]{3,1,2,0:T(8,128)S(1)} %get-tuple-element.16, f32[1,128,8,128]{3,1,2,0:T(8,128)S(1)} %get-tuple-element.17, f32[1,128,8,128]{3,1,2,0:T(8,128)S(1)} %get-tuple-element.15), kind=kLoop, calls=%fused_computation.8 | loop fusion | flops 786432 | bytes 3145728 | tf_op jit(solution)/shard_map/transpose | solution.py:489
  5.0 94.9 %step.1 = (f32[2,6,16,3,8,128]{5,4,3,2,1,0:T(8,128)}, f32[3,8,128,128]{3,2,1,0:T(8,128)}) custom-call(f32[3,8,128,128]{3,2,1,0:T(8,128)} %maximum_bitcast_fusion.refs_0_, bf16[2,192,256]{2,1,0:T(8,128)(2,1)} %constant.76.clone.refs_1_, bf16[2,192,256]{2,1,0:T(8,128)(2,1)} %constant.77.clone.refs_2_, f32[8,128]{1,0:T(8,128)} %constant.78.clone.refs_3_, ...), custom_call_target="tpu_custom_call" | custom-call | tf_op jit(solution)/shard_map/step/pallas_call | solution.py:490
  100.0 2.4 %copy.20 = f32[192,3,8,128]{0,3,2,1:T(8,128)S(1)} copy(f32[192,3,8,128]{3,2,1,0:T(8,128)} %bitcast.54) | data formatting | bytes 4718592 | tf_op jit(solution)/shard_map/reshape | solution.py:515
  102.3 0.0 copy-start.6
  102.4 0.0 copy-start.7
  102.4 0.2 slice_negate_fusion
  102.6 1.2 %copy-done.6 = f32[3,8,128,128]{3,2,1,0:T(8,128)S(1)} copy-done((f32[3,8,128,128]{3,2,1,0:T(8,128)S(1)}, f32[3,8,128,128]{3,2,1,0:T(8,128)}, u32[]{:S(2)}) %copy-start.6) | copy-done | bytes 1572888
  103.8 0.0 copy-done.7
  103.8 2.9 %bitcast_add_fusion = f32[3,128,8,128]{3,1,2,0:T(8,128)S(1)} fusion(f32[3,8,128,128]{3,2,1,0:T(8,128)S(1)} %copy-done.6, f32[128,384,1,1]{1,0,3,2:T(8,128)S(1)} %copy-done.7, f32[192,3,8,64]{0,3,2,1:T(8,128)S(1)} %get-tuple-element.12, f32[192,3,8,64]{0,3,2,1:T(8,128)S(1)} %get-tuple-element.11, f32[192,3,8,128]{0,3,2,1:T(8,128)S(1)} %copy.20), kind=kOutput, calls=%fused_computation.10 | convolution fusion | flops 909115392 | bytes 8060928 | tf_op jit(solution)/shard_map/kx,xfar->fkar/dot_general | solution.py:519
  106.7 0.3 subtract_bitcast_fusion.2
  106.9 0.0 copy-start.1
  107.0 0.0 copy-start.3
  107.0 0.0 copy-start.5
  107.0 0.2 subtract_bitcast_fusion.1
  107.1 0.9 copy-done.1
  108.0 0.2 copy-done.3
  108.1 0.2 copy-done.5
  108.3 1.3 %multiply_subtract_fusion.2 = (f32[1,1,128,8,1,128]{5,2,3,4,1,0:T(8,128)S(1)}, f32[1,1,128,8,1,128]{5,2,3,4,1,0:T(8,128)S(1)}, f32[1,1,128,8,1,128]{5,2,3,4,1,0:T(8,128)}) fusion(f32[1,1,128,8,1,128]{5,4,3,2,1,0:T(1,128)S(1)} %copy-done.1, f32[128]{0:T(128)S(1)} %get-tuple-element.25, f32[128]{0:T(128)S(1)} %fusion.15, f32[128,8]{0,1:T(8,128)S(1)} %broadcast_add_fusion, ...), kind=kLoop, calls=%fused_computation.28 | loop fusion | flops 1835008 | bytes 3151392 | tf_op jit(solution)/shard_map/sub | solution.py:169
  109.6 0.2 multiply_exponential_fusion
  109.8 1.3 %maximum_select_fusion = f32[1,3,128,8,1,128]{5,2,3,4,1,0:T(8,128)S(1)} fusion(f32[1,1,128,8,1,128]{5,2,3,4,1,0:T(8,128)S(1)} %get-tuple-element.19, f32[1,1,128,8,1,128]{5,2,3,4,1,0:T(8,128)} %get-tuple-element.20, f32[1,1,128,8,1,128]{5,2,3,4,1,0:T(8,128)S(1)} %get-tuple-element.18, f32[1,1,128,8,1,128]{5,2,3,4,1,0:T(8,128)S(1)} %get-tuple-element.14, ...), kind=kLoop, calls=%fused_computation.7 | loop fusion | flops 2359296 | bytes 5242881 | tf_op jit(solution)/shard_map/jit(_where)/select_n | solution.py:542
  111.1 2.8 %copy.22 = f32[1,3,128,8,1,128]{5,4,3,2,1,0:T(1,128)} copy(f32[1,3,128,8,1,128]{5,2,3,4,1,0:T(8,128)S(1)} %maximum_select_fusion) | data formatting | bytes 3145728 | tf_op jit(solution)/shard_map/jit(_where)/select_n | solution.py:542
  (5 shorter events, 0.0 us)
Async XLA Ops:
  2.5 0.8 copy-start
  2.6 1.0 copy-start.2
  2.6 1.2 %copy-start.4 = (f32[1,1,128,8,1,128]{5,4,3,2,1,0:T(1,128)}, f32[1,1,128,8,1,128]{5,4,3,2,1,0:T(1,128)S(1)}, u32[]{:S(2)}) copy-start(f32[1,1,128,8,1,128]{5,4,3,2,1,0:T(1,128)S(1)} %get-tuple-element.23) | copy-start | bytes 1572868
  102.3 1.4 %copy-start.6 = (f32[3,8,128,128]{3,2,1,0:T(8,128)S(1)}, f32[3,8,128,128]{3,2,1,0:T(8,128)}, u32[]{:S(2)}) copy-start(f32[3,8,128,128]{3,2,1,0:T(8,128)} %get-tuple-element.7) | copy-start | bytes 4718596
  102.4 1.4 %copy-start.7 = (f32[128,384,1,1]{1,0,3,2:T(8,128)S(1)}, f32[128,384,1,1]{1,0,3,2:T(8,128)}, u32[]{:S(2)}) copy-start(f32[128,384,1,1]{1,0,3,2:T(8,128)} %constant.90) | copy-start | bytes 589828
  106.9 1.0 copy-start.1
  107.0 1.2 %copy-start.3 = (f32[1,1,128,8,1,128]{5,4,3,2,1,0:T(1,128)S(1)}, f32[1,1,128,8,1,128]{5,4,3,2,1,0:T(1,128)}, u32[]{:S(2)}) copy-start(f32[1,1,128,8,1,128]{5,4,3,2,1,0:T(1,128)} %copy-done.2) | copy-start | bytes 1572868
  107.0 1.3 %copy-start.5 = (f32[1,1,128,8,1,128]{5,4,3,2,1,0:T(1,128)S(1)}, f32[1,1,128,8,1,128]{5,4,3,2,1,0:T(1,128)}, u32[]{:S(2)}) copy-start(f32[1,1,128,8,1,128]{5,4,3,2,1,0:T(1,128)} %copy-done.4) | copy-start | bytes 1572868
